TPU v7x, 32 devices: a whole 2x2x4 slice. The times are simulated.
32 devices in a mesh: seq: 4 (over x, core), mp: 8 (over z, y).
Axes of the slice: x: 2, y: 2, z: 4, core: 2. Of those that a mesh axis runs over, the one named last changes fastest.
Arguments:
- byte_states: bfloat16 [4, 4096, 1024], P('seq', 'mp'), may hold values from -312 to 312
- patch_latents: bfloat16 [4, 1024, 4096], P(None, 'seq', 'mp'), may hold values from -6 to 6
- patch_lengths: int32 [4, 1024], P('seq'), may hold values from 1 to 12, 4096 in all within a row
- w_down: bfloat16 [4096, 1024], replicated, may hold values from -0.09375 to 0.09375
- kv_gain: bfloat16 [1024], replicated, may hold values from 0.25 to 1.75
- w_query: bfloat16 [1024, 1024], replicated, may hold values from -0.375 to 0.375
- w_key: bfloat16 [1024, 1024], replicated, may hold values from -0.1875 to 0.1875
- w_value: bfloat16 [1024, 1024], replicated, may hold values from -0.1875 to 0.1875
- w_out: bfloat16 [1024, 1024], replicated, may hold values from -0.375 to 0.375
- out_gain: bfloat16 [1024], replicated, may hold values from 0.25 to 1.75
Outputs:
- decoded: bfloat16 [4, 4096, 1024], P('seq', 'mp')
Inputs may be any that keep to these rules, and one draw needn't show every extreme that they name: patch_lengths[s] lists the lengths of the 1024 patches of sequence s in order; they sum to 4096 and the longest is exactly 12.
All inputs are finite; a program needn't handle non-finite values.
Results may differ from a plain program's by a relative error of at most 0.0076.
Values may be sent and summed in bfloat16 or wider, within the bound.
A program may use at most 128 MiB of HBM per device.

v0:
```python
import math
import jax
import jax.numpy as jnp
from jax import lax
from jax.sharding import PartitionSpec as P

HEADS = 16
HEAD_DIM = 64
NEG_FLOOR = -1e30


def rms_norm(values, gain_row):
    mean_square = jnp.mean(values * values, axis=-1, keepdims=True)
    return values * lax.rsqrt(mean_square + 1e-05) * gain_row.astype(jnp.float32)


def fold_block(fold_state, query_part, position_part, key_block, value_block, start_block):
    row_max, denominator, accumulated = fold_state
    scale_factor = 1.0 / math.sqrt(HEAD_DIM)
    scores = (
        jnp.einsum("rhd,khd->hrk", query_part, key_block, preferred_element_type=jnp.float32)
        * scale_factor
    )
    allowed = start_block[None, None, :] <= position_part[None, :, None]
    masked = jnp.where(allowed, scores, NEG_FLOOR)
    new_max = jnp.maximum(row_max, jnp.max(masked, axis=-1))
    raised = jnp.where(allowed, jnp.exp(masked - new_max[..., None]), 0.0)
    correction = jnp.exp(row_max - new_max)
    denominator = denominator * correction + jnp.sum(raised, axis=-1)
    accumulated = accumulated * correction[..., None] + jnp.einsum(
        "hrk,khd->hrd", raised.astype(jnp.bfloat16), value_block, preferred_element_type=jnp.float32
    )
    return (new_max, denominator, accumulated)


def make_folder(query_halves, position_halves, starts):

    def folder(running, arrived_piece, piece_start):
        key_piece, value_piece = arrived_piece
        piece_rows = key_piece.shape[0]
        step_rows = math.gcd(piece_rows, 512)

        def one_block(block_index, fold_state):
            offset = block_index * step_rows
            key_block = lax.dynamic_slice_in_dim(key_piece, offset, step_rows, 0).reshape(
                step_rows, HEADS, HEAD_DIM
            )
            value_block = lax.dynamic_slice_in_dim(value_piece, offset, step_rows, 0).reshape(
                step_rows, HEADS, HEAD_DIM
            )
            start_block = lax.dynamic_slice_in_dim(starts, offset, step_rows, 0)
            updated = []
            for part_index in range(2):
                part_state = tuple((member[part_index] for member in fold_state))

                def advance(inner_state, part_index=part_index):
                    return fold_block(
                        inner_state,
                        query_halves[part_index],
                        position_halves[part_index],
                        key_block,
                        value_block,
                        start_block,
                    )

                def remain(inner_state):
                    return inner_state

                needed = start_block[0] <= position_halves[part_index][-1]
                updated.append(lax.cond(needed, advance, remain, part_state))
            return tuple((jnp.stack([updated[0][slot], updated[1][slot]]) for slot in range(3)))

        return lax.fori_loop(0, piece_rows // step_rows, one_block, running)

    return folder


def per_device(
    byte_states,
    patch_latents,
    patch_lengths,
    w_down,
    kv_gain,
    w_query,
    w_key,
    w_value,
    w_out,
    out_gain,
):
    my_rank = lax.axis_index("mp")
    tokens_here = byte_states.shape[1]
    half_rows = tokens_here // 2
    regrouped = lax.all_to_all(
        lax.all_to_all(patch_latents, "seq", split_axis=0, concat_axis=1, tiled=True),
        "mp",
        split_axis=1,
        concat_axis=2,
        tiled=True,
    )
    projected = jnp.dot(regrouped[0], w_down, preferred_element_type=jnp.float32)
    patch_normed = rms_norm(projected, kv_gain).astype(jnp.bfloat16)
    lengths = patch_lengths[0]
    starts = jnp.cumsum(lengths) - lengths
    own_rows = byte_states[0]
    local_offsets = jnp.arange(half_rows, dtype=jnp.int32)
    first_position = my_rank * tokens_here
    position_halves = jnp.stack(
        [first_position + local_offsets, first_position + half_rows + local_offsets]
    )
    queries = jnp.dot(own_rows, w_query, preferred_element_type=jnp.float32).astype(jnp.bfloat16)
    query_halves = queries.reshape(2, half_rows, HEADS, HEAD_DIM)
    initial = (
        jnp.full((2, HEADS, half_rows), NEG_FLOOR, jnp.float32),
        jnp.zeros((2, HEADS, half_rows), jnp.float32),
        jnp.zeros((2, HEADS, half_rows, HEAD_DIM), jnp.float32),
    )
    key_rows = jnp.dot(patch_normed, w_key, preferred_element_type=jnp.float32).astype(jnp.bfloat16)
    value_rows = jnp.dot(patch_normed, w_value, preferred_element_type=jnp.float32).astype(
        jnp.bfloat16
    )
    folder = make_folder(query_halves, position_halves, starts)
    row_max, denominator, accumulated = folder(
        initial,
        (
            lax.all_gather(key_rows, "mp", axis=0, tiled=True),
            lax.all_gather(value_rows, "mp", axis=0, tiled=True),
        ),
        jnp.int32(0),
    )
    summed = accumulated / denominator[..., None]
    head_out = (
        jnp.transpose(summed, (0, 2, 1, 3))
        .reshape(tokens_here, HEADS * HEAD_DIM)
        .astype(jnp.bfloat16)
    )
    residual = own_rows.astype(jnp.float32) + jnp.dot(
        head_out, w_out, preferred_element_type=jnp.float32
    )
    decoded = rms_norm(residual, out_gain).astype(jnp.bfloat16)
    return decoded[None]


def solution(mesh):
    return jax.shard_map(
        per_device,
        mesh=mesh,
        in_specs=(
            P("seq", "mp", None),
            P(None, "seq", "mp"),
            P("seq", None),
            P(),
            P(),
            P(),
            P(),
            P(),
            P(),
            P(),
        ),
        out_specs=P("seq", "mp", None),
        check_vma=False,
    )
```

profile of v0, /device:TPU:16, one launch (start us, length us, event | category | flops | bytes accessed | tf_op | source)
XLA Modules:
  0.0 283.9 jit_solution(9395675272807082795)
XLA Ops:
  6.5 18.0 %all_to_all.27 = bf16[4,256,512]{2,1,0:T(8,128)(2,1)S(1)} all-to-all(bf16[4,256,512]{2,1,0:T(8,128)(2,1)} %param.17), channel_id=1, replica_groups=mesh['seq'=4,'mp'=8] {'seq'}, dimensions={0} | all-to-all | bytes 2097152 | tf_op jit(solution)/shard_map/all_to_all | solution.py:94
  24.6 3.0 %copy.45 = bf16[1,1024,512]{2,0,1:T(2,128)(2,1)} copy(bf16[1,1024,512]{2,1,0:T(8,128)(2,1)S(1)} %bitcast.101) | data formatting | bytes 2097152 | tf_op jit(solution)/shard_map/all_to_all | solution.py:94
  28.1 8.0 %reduce.2 = bf16[1024,512]{1,0:T(8,128)(2,1)S(1)} reduce(bf16[1024,1,512]{2,1,0:T(2,128)(2,1)} %bitcast.98, bf16[]{:T(256)} %broadcast.104), dimensions={1}, to_apply=%bitcast.78.reduce_sub_computation | reduce | bytes 2097154
  37.7 6.2 %all-to-all-start.1 = ((bf16[8,2,32768]{2,1,0:T(2,128)(2,1)}), bf16[8,2,32768]{2,1,0:T(2,128)(2,1)S(1)}, u32[]{:S(2)}, u32[]{:S(2)}) async-start(bf16[8,2,32768]{2,1,0:T(2,128)(2,1)} %reshape.138), calls=%async_computation.1 | async-start | bytes 2097152 | tf_op jit(solution)/shard_map/all_to_all | solution.py:93
  43.9 22.3 %all-to-all-done.1 = bf16[8,2,32768]{2,1,0:T(2,128)(2,1)S(1)} async-done(((bf16[8,2,32768]{2,1,0:T(2,128)(2,1)}), bf16[8,2,32768]{2,1,0:T(2,128)(2,1)S(1)}, u32[]{:S(2)}, u32[]{:S(2)}) %all-to-all-start.1) | async-done | bytes 1048608 | tf_op jit(solution)/shard_map/all_to_all | solution.py:93
  66.1 3.4 %reshape.139 = bf16[1024,1,512]{2,1,0:T(2,128)(2,1)} reshape(bf16[8,2,32768]{2,1,0:T(2,128)(2,1)S(1)} %all-to-all-done.1) | data formatting | bytes 2097152
  74.0 4.9 %multiply_reduce_fusion.1 = (f32[128]{0:T(128)S(1)}, f32[128,1024]{1,0:T(8,128)S(1)}) fusion(bf16[128,4096]{0,1:T(8,128)(2,1)S(1)} %bitcast.99, bf16[4096,1024]{1,0:T(8,128)(2,1)} %param.19), kind=kOutput, calls=%fused_computation.58 | convolution fusion | flops 1074003840 | bytes 9961984 | tf_op jit(solution)/shard_map/dot_general | solution.py:100
  81.2 3.0 %convolution_convert_fusion.1 = bf16[128,1024]{1,0:T(8,128)(2,1)} fusion(bf16[1024,1024]{1,0:T(8,128)(2,1)} %param.23, f32[128,1024]{1,0:T(8,128)} %copy-done.7, f32[1024]{0:T(1024)S(1)} %convert_element_type.60, f32[128]{0:T(128)S(1)} %add_rsqrt_fusion.1), kind=kOutput, calls=%fused_computation.52 | convolution fusion | flops 268959744 | bytes 2888192 | tf_op jit(solution)/shard_map/dot_general | solution.py:118
  84.6 3.2 %convolution_convert_fusion = bf16[512,1024]{1,0:T(8,128)(2,1)S(1)} fusion(bf16[1024,1024]{1,0:T(8,128)(2,1)} %param.21, bf16[1,512,1024]{2,1,0:T(8,128)(2,1)} %param.16), kind=kOutput, calls=%fused_computation.51 | convolution fusion | flops 1074266112 | bytes 4194304 | tf_op jit(solution)/shard_map/dot_general | solution.py:110
  90.1 3.6 %copy.36 = bf16[2,256,16,64]{1,3,2,0:T(8,128)(2,1)} copy(bf16[2,256,16,64]{3,2,1,0:T(8,128)(2,1)} %reshape.136) | data formatting | bytes 2097152 | tf_op jit(solution)/shard_map/while | solution.py:73
  93.8 36.8 %all-gather.3.cloned.1.call-done = bf16[1024,1024]{1,0:T(8,128)(2,1)} async-done(((bf16[128,1024]{1,0:T(8,128)(2,1)}), bf16[1024,1024]{1,0:T(8,128)(2,1)}) %all-gather.3.cloned.1.call-update) | async-done | bytes 2097168 | tf_op jit(solution)/shard_map/all_gather | solution.py:125
  130.6 49.8 %all-gather.5.cloned.1.call-done = bf16[1024,1024]{1,0:T(8,128)(2,1)} async-done(((bf16[128,1024]{1,0:T(8,128)(2,1)}), bf16[1024,1024]{1,0:T(8,128)(2,1)}) %all-gather.5.cloned.1.call-update) | async-done | bytes 2097168 | tf_op jit(solution)/shard_map/all_gather | solution.py:126
  182.0 88.0 %while.17 = (s32[]{:T(128)}, f32[2,16,256]{2,1,0:T(8,128)S(1)}, f32[2,16,256]{2,1,0:T(8,128)S(1)}, f32[2,16,256,64]{2,3,1,0:T(8,128)}, s32[1024]{0:T(1024)S(1)},...) while((s32[]{:T(128)}, f32[2,16,256]{2,1,0:T(8,128)S(1)}, ...), condition=%wide.region_12.13_spmd, body=%wide.region_3.12_spmd.sunk | while | flops 1130135552 | bytes 103557752 | solution.py:73
  185.2 3.1 %slice_bitcast_fusion.9 = (f32[16,256,64]{1,2,0:T(8,128)}, f32[16,256,64]{1,2,0:T(8,128)}) fusion(f32[2,16,256,64]{2,3,1,0:T(8,128)} %get-tuple-element.503), kind=kLoop, calls=%fused_computation.38.clone.1 | loop fusion | bytes 4194304 | tf_op jit(solution)/shard_map/while/body/eval_jaxpr/squeeze | solution.py:54
  188.3 3.0 %constant_dynamic-slice_fusion.3 = (bf16[512,1024]{1,0:T(8,128)(2,1)}, bf16[512,1024]{1,0:T(8,128)(2,1)}) fusion(bf16[1024,1024]{1,0:T(8,128)(2,1)} %get-tuple-element.521, s32[]{:T(128)S(6)} %select_n.71, bf16[1024,1024]{1,0:T(8,128)(2,1)} %get-tuple-element.520), kind=kLoop, calls=%fused_computation.45.clone.1 | loop fusion | bytes 4194308 | tf_op jit(solution)/shard_map/while/body/eval_jaxpr/dynamic_slice | solution.py:48
  195.8 11.8 %conditional.4 = (f32[1,16,256]{2,1,0:T(8,128)}, f32[1,16,256]{2,1,0:T(8,128)S(1)}, f32[1,16,256,64]{2,3,1,0:T(8,128)}) conditional(s32[]{:T(128)} %bitcast.87, (f32[16,256]{1,0:T(8,128)}, f32[16,256]{1,0:T(8,128)S(1)}, f32[16,256,64]{1,2,0:T(8,128)}) %tuple.129, (s32[512]{0:T(512)S(1)}, s32[256]{0:T(256)S(1)}, bf16[2,256,16,64]{1,3,2,0:T(8,128)(2,1)}, ...), branch_computations={%region_8.8_spmd, %region_9.0_spmd} | conditional | flops 564797440 | bytes 43224172 | solution.py:70
  199.5 3.2 %fusion.20 = f32[16,256]{1,0:T(8,128)S(1)} fusion(f32[16,256,512]{2,1,0:T(8,128)S(1)} %get-tuple-element.368, f32[16,256]{1,0:T(8,128)} %max.5, pred[256,512]{1,0:T(8,128)(4,1)S(1)} %broadcast_compare_fusion.1), kind=kLoop, calls=%fused_computation.22 | loop fusion | flops 10481664 | bytes 8552448 | tf_op jit(solution)/shard_map/while/body/eval_jaxpr/cond/branch_1_fun/reduce_sum | solution.py:29
  203.5 3.1 %fusion.27 = f32[1,16,256,64]{2,3,1,0:T(8,128)S(1)} fusion(bf16[512,16,64]{0,2,1:T(8,128)(2,1)S(1)} %copy-done.5, f32[16,256,512]{2,1,0:T(8,128)S(1)} %get-tuple-element.368, f32[16,256]{1,0:T(8,128)} %max.5, pred[256,512]{1,0:T(8,128)(4,1)S(1)} %broadcast_compare_fusion.1, f32[16,256,64]{1,2,0:T(8,128)S(1)} %copy-done.3, f32[16,256]{1,0:T(8,128)S(1)} %get-tuple-element.364), kind=kOutput, calls=%fused_computation.26 | convolution fusion | flops 279445504 | bytes 11698176 | tf_op jit(solution)/shard_map/while/body/eval_jaxpr/cond/branch_1_fun/hrk,khd->hrd/dot_general | solution.py:30
  210.3 11.8 %conditional.5 = (f32[1,16,256]{2,1,0:T(8,128)}, f32[1,16,256]{2,1,0:T(8,128)S(1)}, f32[1,16,256,64]{2,3,1,0:T(8,128)}) conditional(s32[]{:T(128)} %bitcast.90, (f32[16,256]{1,0:T(8,128)}, f32[16,256]{1,0:T(8,128)S(1)}, f32[16,256,64]{1,2,0:T(8,128)}) %tuple.131, (s32[512]{0:T(512)S(1)}, s32[256]{0:T(256)S(1)}, bf16[2,256,16,64]{1,3,2,0:T(8,128)(2,1)}, ...), branch_computations={%region_4.4_spmd, %region_5.0_spmd} | conditional | flops 564797440 | bytes 43224172 | solution.py:70
  214.0 3.2 %fusion.2 = f32[16,256]{1,0:T(8,128)S(1)} fusion(f32[16,256,512]{2,1,0:T(8,128)S(1)} %get-tuple-element.366, f32[16,256]{1,0:T(8,128)} %max.4, pred[256,512]{1,0:T(8,128)(4,1)S(1)} %broadcast_compare_fusion), kind=kLoop, calls=%fused_computation.4 | loop fusion | flops 10481664 | bytes 8552448 | tf_op jit(solution)/shard_map/while/body/eval_jaxpr/cond/branch_1_fun/reduce_sum | solution.py:29
  218.0 3.1 %fusion.9 = f32[1,16,256,64]{2,3,1,0:T(8,128)S(1)} fusion(bf16[512,16,64]{0,2,1:T(8,128)(2,1)S(1)} %copy-done.6, f32[16,256,512]{2,1,0:T(8,128)S(1)} %get-tuple-element.366, f32[16,256]{1,0:T(8,128)} %max.4, pred[256,512]{1,0:T(8,128)(4,1)S(1)} %broadcast_compare_fusion, f32[16,256,64]{1,2,0:T(8,128)S(1)} %copy-done.1, f32[16,256]{1,0:T(8,128)S(1)} %get-tuple-element.362), kind=kOutput, calls=%fused_computation.8 | convolution fusion | flops 279445504 | bytes 11698176 | tf_op jit(solution)/shard_map/while/body/eval_jaxpr/cond/branch_1_fun/hrk,khd->hrd/dot_general | solution.py:30
  222.9 3.1 %pad_maximum_fusion.8 = f32[2,16,256,64]{2,3,1,0:T(8,128)} fusion(f32[1,16,256,64]{2,3,1,0:T(8,128)} %get-tuple-element.472, f32[1,16,256,64]{2,3,1,0:T(8,128)} %get-tuple-element.473), kind=kLoop, calls=%fused_computation.36.clone.1 | loop fusion | flops 524288 | bytes 4194304 | tf_op jit(solution)/shard_map/while/body/eval_jaxpr/stack | solution.py:71
  229.2 3.1 %slice_bitcast_fusion.9 = (f32[16,256,64]{1,2,0:T(8,128)}, f32[16,256,64]{1,2,0:T(8,128)}) fusion(f32[2,16,256,64]{2,3,1,0:T(8,128)} %get-tuple-element.503), kind=kLoop, calls=%fused_computation.38.clone.1 | loop fusion | bytes 4194304 | tf_op jit(solution)/shard_map/while/body/eval_jaxpr/squeeze | solution.py:54
  232.3 3.0 %constant_dynamic-slice_fusion.3 = (bf16[512,1024]{1,0:T(8,128)(2,1)}, bf16[512,1024]{1,0:T(8,128)(2,1)}) fusion(bf16[1024,1024]{1,0:T(8,128)(2,1)} %get-tuple-element.521, s32[]{:T(128)S(6)} %select_n.71, bf16[1024,1024]{1,0:T(8,128)(2,1)} %get-tuple-element.520), kind=kLoop, calls=%fused_computation.45.clone.1 | loop fusion | bytes 4194308 | tf_op jit(solution)/shard_map/while/body/eval_jaxpr/dynamic_slice | solution.py:48
  239.8 11.8 %conditional.4 = (f32[1,16,256]{2,1,0:T(8,128)}, f32[1,16,256]{2,1,0:T(8,128)S(1)}, f32[1,16,256,64]{2,3,1,0:T(8,128)}) conditional(s32[]{:T(128)} %bitcast.87, (f32[16,256]{1,0:T(8,128)}, f32[16,256]{1,0:T(8,128)S(1)}, f32[16,256,64]{1,2,0:T(8,128)}) %tuple.129, (s32[512]{0:T(512)S(1)}, s32[256]{0:T(256)S(1)}, bf16[2,256,16,64]{1,3,2,0:T(8,128)(2,1)}, ...), branch_computations={%region_8.8_spmd, %region_9.0_spmd} | conditional | flops 564797440 | bytes 43224172 | solution.py:70
  240.0 2.9 %fusion.18 = (f32[16,256]{1,0:T(8,128)S(1)}, f32[16,256,512]{2,1,0:T(8,128)S(1)}) fusion(pred[256,512]{1,0:T(8,128)(4,1)S(1)} %broadcast_compare_fusion.1, bf16[512,16,64]{0,2,1:T(8,128)(2,1)S(1)} %get-tuple-element.254, bf16[2,256,16,64]{1,3,2,0:T(8,128)(2,1)} %get-tuple-element.253), kind=kOutput, calls=%fused_computation.20 | convolution fusion | flops 274722816 | bytes 10108928 | tf_op jit(solution)/shard_map/while/body/eval_jaxpr/cond/branch_1_fun/rhd,khd->hrk/dot_general | solution.py:21
  243.5 3.2 %fusion.20 = f32[16,256]{1,0:T(8,128)S(1)} fusion(f32[16,256,512]{2,1,0:T(8,128)S(1)} %get-tuple-element.368, f32[16,256]{1,0:T(8,128)} %max.5, pred[256,512]{1,0:T(8,128)(4,1)S(1)} %broadcast_compare_fusion.1), kind=kLoop, calls=%fused_computation.22 | loop fusion | flops 10481664 | bytes 8552448 | tf_op jit(solution)/shard_map/while/body/eval_jaxpr/cond/branch_1_fun/reduce_sum | solution.py:29
  247.5 3.1 %fusion.27 = f32[1,16,256,64]{2,3,1,0:T(8,128)S(1)} fusion(bf16[512,16,64]{0,2,1:T(8,128)(2,1)S(1)} %copy-done.5, f32[16,256,512]{2,1,0:T(8,128)S(1)} %get-tuple-element.368, f32[16,256]{1,0:T(8,128)} %max.5, pred[256,512]{1,0:T(8,128)(4,1)S(1)} %broadcast_compare_fusion.1, f32[16,256,64]{1,2,0:T(8,128)S(1)} %copy-done.3, f32[16,256]{1,0:T(8,128)S(1)} %get-tuple-element.364), kind=kOutput, calls=%fused_computation.26 | convolution fusion | flops 279445504 | bytes 11698176 | tf_op jit(solution)/shard_map/while/body/eval_jaxpr/cond/branch_1_fun/hrk,khd->hrd/dot_general | solution.py:30
  254.3 11.8 %conditional.5 = (f32[1,16,256]{2,1,0:T(8,128)}, f32[1,16,256]{2,1,0:T(8,128)S(1)}, f32[1,16,256,64]{2,3,1,0:T(8,128)}) conditional(s32[]{:T(128)} %bitcast.90, (f32[16,256]{1,0:T(8,128)}, f32[16,256]{1,0:T(8,128)S(1)}, f32[16,256,64]{1,2,0:T(8,128)}) %tuple.131, (s32[512]{0:T(512)S(1)}, s32[256]{0:T(256)S(1)}, bf16[2,256,16,64]{1,3,2,0:T(8,128)(2,1)}, ...), branch_computations={%region_4.4_spmd, %region_5.0_spmd} | conditional | flops 564797440 | bytes 43224172 | solution.py:70
  258.0 3.2 %fusion.2 = f32[16,256]{1,0:T(8,128)S(1)} fusion(f32[16,256,512]{2,1,0:T(8,128)S(1)} %get-tuple-element.366, f32[16,256]{1,0:T(8,128)} %max.4, pred[256,512]{1,0:T(8,128)(4,1)S(1)} %broadcast_compare_fusion), kind=kLoop, calls=%fused_computation.4 | loop fusion | flops 10481664 | bytes 8552448 | tf_op jit(solution)/shard_map/while/body/eval_jaxpr/cond/branch_1_fun/reduce_sum | solution.py:29
  262.0 3.1 %fusion.9 = f32[1,16,256,64]{2,3,1,0:T(8,128)S(1)} fusion(bf16[512,16,64]{0,2,1:T(8,128)(2,1)S(1)} %copy-done.6, f32[16,256,512]{2,1,0:T(8,128)S(1)} %get-tuple-element.366, f32[16,256]{1,0:T(8,128)} %max.4, pred[256,512]{1,0:T(8,128)(4,1)S(1)} %broadcast_compare_fusion, f32[16,256,64]{1,2,0:T(8,128)S(1)} %copy-done.1, f32[16,256]{1,0:T(8,128)S(1)} %get-tuple-element.362), kind=kOutput, calls=%fused_computation.8 | convolution fusion | flops 279445504 | bytes 11698176 | tf_op jit(solution)/shard_map/while/body/eval_jaxpr/cond/branch_1_fun/hrk,khd->hrd/dot_general | solution.py:30
  266.9 3.1 %pad_maximum_fusion.8 = f32[2,16,256,64]{2,3,1,0:T(8,128)} fusion(f32[1,16,256,64]{2,3,1,0:T(8,128)} %get-tuple-element.472, f32[1,16,256,64]{2,3,1,0:T(8,128)} %get-tuple-element.473), kind=kLoop, calls=%fused_computation.36.clone.1 | loop fusion | flops 524288 | bytes 4194304 | tf_op jit(solution)/shard_map/while/body/eval_jaxpr/stack | solution.py:71
  (101 shorter events, 56.0 us)
Async XLA Ops:
  6.5 266.6 %copy-start = (bf16[1024,1024]{1,0:T(8,128)(2,1)S(1)}, bf16[1024,1024]{1,0:T(8,128)(2,1)}, u32[]{:S(2)}) copy-start(bf16[1024,1024]{1,0:T(8,128)(2,1)} %param.24) | copy-start | bytes 6291460
  6.5 37.3 %copy-start.10 = (bf16[1024]{0:T(1024)(128)(2,1)S(1)}, bf16[1024]{0:T(1024)(128)(2,1)}, u32[]{:S(2)}) copy-start(bf16[1024]{0:T(1024)(128)(2,1)} %param.20) | copy-start | bytes 6148
  37.7 28.5 %all-to-all-start.1 = ((bf16[8,2,32768]{2,1,0:T(2,128)(2,1)}), bf16[8,2,32768]{2,1,0:T(2,128)(2,1)S(1)}, u32[]{:S(2)}, u32[]{:S(2)}) async-start(bf16[8,2,32768]{2,1,0:T(2,128)(2,1)} %reshape.138), calls=%async_computation.1 | async-start | bytes 2097152 | tf_op jit(solution)/shard_map/all_to_all | solution.py:93
  43.9 86.8 %all-gather.3.cloned.1.call-start = ((), (), s32[]{:S(2)}) async-start(), calls=%async_computation.2 | async-start | bytes 2359296 | tf_op jit(solution)/shard_map/all_gather | solution.py:125
  74.0 5.7 %copy-start.8 = (bf16[1024,1024]{1,0:T(8,128)(2,1)S(1)}, bf16[1024,1024]{1,0:T(8,128)(2,1)}, u32[]{:S(2)}) copy-start(bf16[1024,1024]{1,0:T(8,128)(2,1)} %param.22) | copy-start | bytes 6291460
  74.0 10.1 %copy-start.9 = (s32[1,1024]{1,0:T(1,128)S(1)}, s32[1,1024]{1,0:T(1,128)}, u32[]{:S(2)}) copy-start(s32[1,1024]{1,0:T(1,128)} %param.18) | copy-start | bytes 12292
  78.9 0.8 copy-start.7
  80.9 12.7 %copy-start.11 = (bf16[1024]{0:T(1024)(128)(2,1)S(1)}, bf16[1024]{0:T(1024)(128)(2,1)}, u32[]{:S(2)}) copy-start(bf16[1024]{0:T(1024)(128)(2,1)} %param.25) | copy-start | bytes 6148
  80.9 99.5 %all-gather.5.cloned.1.call-start = ((), (), s32[]{:S(2)}) async-start(), calls=%async_computation.3 | async-start | bytes 2359296 | tf_op jit(solution)/shard_map/all_gather | solution.py:126
  195.9 7.5 %copy-start.3 = (f32[16,256,64]{1,2,0:T(8,128)S(1)}, f32[16,256,64]{1,2,0:T(8,128)}, u32[]{:S(2)}) copy-start(f32[16,256,64]{1,2,0:T(8,128)} %get-tuple-element.256) | copy-start | bytes 3145732 | tf_op jit(solution)/shard_map/while/body/eval_jaxpr/cond
  196.0 7.5 %copy-start.5 = (bf16[512,16,64]{0,2,1:T(8,128)(2,1)S(1)}, bf16[512,16,64]{0,2,1:T(8,128)(2,1)}, u32[]{:S(2)}) copy-start(bf16[512,16,64]{0,2,1:T(8,128)(2,1)} %get-tuple-element.257) | copy-start | bytes 3145732 | tf_op jit(solution)/shard_map/while/body/eval_jaxpr/cond
  206.6 1.0 copy-start.4
  210.5 7.5 %copy-start.1 = (f32[16,256,64]{1,2,0:T(8,128)S(1)}, f32[16,256,64]{1,2,0:T(8,128)}, u32[]{:S(2)}) copy-start(f32[16,256,64]{1,2,0:T(8,128)} %get-tuple-element.248) | copy-start | bytes 3145732 | tf_op jit(solution)/shard_map/while/body/eval_jaxpr/cond
  210.5 7.5 %copy-start.6 = (bf16[512,16,64]{0,2,1:T(8,128)(2,1)S(1)}, bf16[512,16,64]{0,2,1:T(8,128)(2,1)}, u32[]{:S(2)}) copy-start(bf16[512,16,64]{0,2,1:T(8,128)(2,1)} %get-tuple-element.249) | copy-start | bytes 3145732 | tf_op jit(solution)/shard_map/while/body/eval_jaxpr/cond
  221.2 1.0 copy-start.2
  240.0 7.5 %copy-start.3 = (f32[16,256,64]{1,2,0:T(8,128)S(1)}, f32[16,256,64]{1,2,0:T(8,128)}, u32[]{:S(2)}) copy-start(f32[16,256,64]{1,2,0:T(8,128)} %get-tuple-element.256) | copy-start | bytes 3145732 | tf_op jit(solution)/shard_map/while/body/eval_jaxpr/cond
  240.0 7.5 %copy-start.5 = (bf16[512,16,64]{0,2,1:T(8,128)(2,1)S(1)}, bf16[512,16,64]{0,2,1:T(8,128)(2,1)}, u32[]{:S(2)}) copy-start(bf16[512,16,64]{0,2,1:T(8,128)(2,1)} %get-tuple-element.257) | copy-start | bytes 3145732 | tf_op jit(solution)/shard_map/while/body/eval_jaxpr/cond
  250.7 1.0 copy-start.4
  254.5 7.5 %copy-start.1 = (f32[16,256,64]{1,2,0:T(8,128)S(1)}, f32[16,256,64]{1,2,0:T(8,128)}, u32[]{:S(2)}) copy-start(f32[16,256,64]{1,2,0:T(8,128)} %get-tuple-element.248) | copy-start | bytes 3145732 | tf_op jit(solution)/shard_map/while/body/eval_jaxpr/cond
  254.5 7.5 %copy-start.6 = (bf16[512,16,64]{0,2,1:T(8,128)(2,1)S(1)}, bf16[512,16,64]{0,2,1:T(8,128)(2,1)}, u32[]{:S(2)}) copy-start(bf16[512,16,64]{0,2,1:T(8,128)(2,1)} %get-tuple-element.249) | copy-start | bytes 3145732 | tf_op jit(solution)/shard_map/while/body/eval_jaxpr/cond
  265.2 1.0 copy-start.2
Sparse Core Ops, SparseCore 0:
  81.1 49.5 all-gather.2
  132.7 47.6 all-gather.4
where the time goes:
time: 286 us; the launch traced here: 284 us
  waiting for transfers between devices  109 us (38%)
  local copies, waits for them, and re-layouts  54.5 us (19%)
  matrix products  39.1 us (14%)
  other arithmetic  38 us (13%)
  blocking collectives  18 us (6%)
  between operations  13.5 us (5%)
  starting transfers between devices  6.39 us (2%)
  loops' own time  5.51 us (2%)
    all_gather x1, waiting for transfers between devices, per_device(): lax.all_gather(value_rows, 'mp', axis=0, tiled=True)  49.8 us
    all_gather x1, waiting for transfers between devices, per_device(): lax.all_gather(key_rows, 'mp', axis=0, tiled=True)  36.8 us
    all_to_all x1, waiting for transfers between devices, per_device(): lax.all_to_all(lax.all_to_all(patch_latents, 'seq', split_axis=0, concat_...  22.3 us
    all_to_all x1, blocking collectives, per_device(): lax.all_to_all(patch_latents, 'seq', split_axis=0, concat_axis=1, tiled=T...  18 us
    reduce_sum x4, other arithmetic, fold_block(): denominator = denominator * correction + jnp.sum(raised, axis=-1)  12.9 us
    dot_general x4, matrix products, fold_block(): jnp.einsum('hrk,khd->hrd', raised.astype(jnp.bfloat16), value_block, pref...  12.6 us
    dot_general x4, matrix products, fold_block(): jnp.einsum('rhd,khd->hrk', query_part, key_block, preferred_element_type=...  11.7 us
    another operation x10, other arithmetic, one_block(): jnp.stack([updated[0][slot], updated[1][slot]])  10.6 us
  transfers between devices with their start and end apart: 3, of which 3 were waited for; matrix products, arithmetic and copies ran while one was open for 4% of the time, Pallas kernels for 0%

commit v1 on v0

--- a/solution.py
+++ b/solution.py
@@ -90,13 +90,10 @@
     my_rank = lax.axis_index("mp")
     tokens_here = byte_states.shape[1]
     half_rows = tokens_here // 2
-    regrouped = lax.all_to_all(
-        lax.all_to_all(patch_latents, "seq", split_axis=0, concat_axis=1, tiled=True),
-        "mp",
-        split_axis=1,
-        concat_axis=2,
-        tiled=True,
-    )
+    part = lax.all_to_all(patch_latents, "seq", split_axis=0, concat_axis=1, tiled=True)
+    pieces = jnp.split(part, lax.axis_size("mp"), axis=1)
+    arrived = lax.all_to_all(jnp.stack(pieces), "mp", 0, 0)
+    regrouped = jnp.concatenate(arrived, axis=2)
     projected = jnp.dot(regrouped[0], w_down, preferred_element_type=jnp.float32)
     patch_normed = rms_norm(projected, kv_gain).astype(jnp.bfloat16)
     lengths = patch_lengths[0]

time: 286 us -> 270 us (0.944)
  other arithmetic: 38 us -> 30 us
  local copies, waits for them, and re-layouts: 54.5 us -> 47.6 us
    unnamed x1 -> x0, other arithmetic: 8.04 us -> none
    all_to_all x2 -> x0, local copies, waits for them, and re-layouts: 4.58 us -> none  [the longest x1 2.97 us: per_device(): lax.all_to_all(patch_latents, 'seq', split_axis=0, concat_axis=1, tiled=T...]
    unnamed x17 -> x28, local copies, waits for them, and re-layouts: 9.39 us -> 6.67 us
  transfers between devices with their start and end apart: 3 -> 3, of which waited for: 3 -> 3; matrix products, arithmetic and copies ran while one was open for 4% -> 5% of each run, Pallas kernels for 0% -> 0%
where the time goes in v1:
time: 270 us; the launch traced here: 269 us
  waiting for transfers between devices  109 us (40%)
  local copies, waits for them, and re-layouts  47.6 us (18%)
  matrix products  39.1 us (14%)
  other arithmetic  30 us (11%)
  blocking collectives  18 us (7%)
  between operations  13.6 us (5%)
  starting transfers between devices  6.21 us (2%)
  loops' own time  5.03 us (2%)
    all_gather x1, waiting for transfers between devices, per_device(): lax.all_gather(value_rows, 'mp', axis=0, tiled=True)  49.8 us
    all_gather x1, waiting for transfers between devices, per_device(): lax.all_gather(key_rows, 'mp', axis=0, tiled=True)  37 us
    all_to_all x1, waiting for transfers between devices, per_device(): arrived = lax.all_to_all(jnp.stack(pieces), 'mp', 0, 0)  22.3 us
    all_to_all x1, blocking collectives, per_device(): lax.all_to_all(patch_latents, 'seq', split_axis=0, concat_axis=1, tiled=T...  18 us
    reduce_sum x4, other arithmetic, fold_block(): denominator = denominator * correction + jnp.sum(raised, axis=-1)  12.9 us
    dot_general x4, matrix products, fold_block(): jnp.einsum('hrk,khd->hrd', raised.astype(jnp.bfloat16), value_block, pref...  12.6 us
    dot_general x4, matrix products, fold_block(): jnp.einsum('rhd,khd->hrk', query_part, key_block, preferred_element_type=...  11.7 us
    another operation x10, other arithmetic, one_block(): jnp.stack([updated[0][slot], updated[1][slot]])  10.6 us
  transfers between devices with their start and end apart: 3, of which 3 were waited for; matrix products, arithmetic and copies ran while one was open for 5% of the time, Pallas kernels for 0%

profile of v1, /device:TPU:16, one launch (start us, length us, event | category | flops | bytes accessed | tf_op | source)
XLA Modules:
  0.0 268.6 jit_solution(9041626697205601930)
XLA Ops:
  6.5 18.0 %all_to_all.17 = bf16[4,256,512]{2,1,0:T(8,128)(2,1)S(1)} all-to-all(bf16[4,256,512]{2,1,0:T(8,128)(2,1)} %param.17), channel_id=1, replica_groups=mesh['seq'=4,'mp'=8] {'seq'}, dimensions={0} | all-to-all | bytes 2097152 | tf_op jit(solution)/shard_map/all_to_all | solution.py:93
  31.0 6.2 %all-to-all-start.1 = ((bf16[8,1,128,512]{2,3,1,0:T(8,128)(2,1)}), bf16[8,1,128,512]{2,3,1,0:T(8,128)(2,1)S(1)}, u32[]{:S(2)}, u32[]{:S(2)}) async-start(bf16[8,1,128,512]{2,3,1,0:T(8,128)(2,1)} %bitcast_dynamic-update-slice_fusion), calls=%async_computation.1 | async-start | bytes 2097152 | tf_op jit(solution)/shard_map/all_to_all | solution.py:95
  37.2 22.3 %all-to-all-done.1 = bf16[8,1,128,512]{2,3,1,0:T(8,128)(2,1)S(1)} async-done(((bf16[8,1,128,512]{2,3,1,0:T(8,128)(2,1)}), bf16[8,1,128,512]{2,3,1,0:T(8,128)(2,1)S(1)}, u32[]{:S(2)}, u32[]{:S(2)}) %all-to-all-start.1) | async-done | bytes 1048608 | tf_op jit(solution)/shard_map/all_to_all | solution.py:95
  59.5 4.9 %multiply_reduce_fusion.1 = (f32[128]{0:T(128)S(1)}, f32[128,1024]{1,0:T(8,128)S(1)}) fusion(bf16[128,4096]{0,1:T(8,128)(2,1)S(1)} %bitcast.110, bf16[4096,1024]{1,0:T(8,128)(2,1)} %param.19), kind=kOutput, calls=%fused_computation.58 | convolution fusion | flops 1074003840 | bytes 9961984 | tf_op jit(solution)/shard_map/dot_general | solution.py:97
  66.5 3.0 %convolution_convert_fusion.1 = bf16[128,1024]{1,0:T(8,128)(2,1)} fusion(bf16[1024,1024]{1,0:T(8,128)(2,1)} %param.23, f32[128,1024]{1,0:T(8,128)} %copy-done.7, f32[1024]{0:T(1024)S(1)} %convert_element_type.60, f32[128]{0:T(128)S(1)} %add_rsqrt_fusion.1), kind=kOutput, calls=%fused_computation.52 | convolution fusion | flops 268959744 | bytes 2888192 | tf_op jit(solution)/shard_map/dot_general | solution.py:115
  69.9 3.2 %convolution_convert_fusion = bf16[512,1024]{1,0:T(8,128)(2,1)S(1)} fusion(bf16[1024,1024]{1,0:T(8,128)(2,1)} %param.21, bf16[1,512,1024]{2,1,0:T(8,128)(2,1)} %param.16), kind=kOutput, calls=%fused_computation.51 | convolution fusion | flops 1074266112 | bytes 4194304 | tf_op jit(solution)/shard_map/dot_general | solution.py:107
  75.4 3.6 %copy.32 = bf16[2,256,16,64]{1,3,2,0:T(8,128)(2,1)} copy(bf16[2,256,16,64]{3,2,1,0:T(8,128)(2,1)} %reshape.139) | data formatting | bytes 2097152 | tf_op jit(solution)/shard_map/while | solution.py:73
  79.1 37.0 %all-gather.3.cloned.1.call-done = bf16[1024,1024]{1,0:T(8,128)(2,1)} async-done(((bf16[128,1024]{1,0:T(8,128)(2,1)}), bf16[1024,1024]{1,0:T(8,128)(2,1)}) %all-gather.3.cloned.1.call-update) | async-done | bytes 2097168 | tf_op jit(solution)/shard_map/all_gather | solution.py:122
  116.1 49.8 %all-gather.5.cloned.1.call-done = bf16[1024,1024]{1,0:T(8,128)(2,1)} async-done(((bf16[128,1024]{1,0:T(8,128)(2,1)}), bf16[1024,1024]{1,0:T(8,128)(2,1)}) %all-gather.5.cloned.1.call-update) | async-done | bytes 2097168 | tf_op jit(solution)/shard_map/all_gather | solution.py:123
  167.4 87.2 %while.17 = (s32[]{:T(128)}, f32[2,16,256]{2,1,0:T(8,128)S(1)}, f32[2,16,256]{2,1,0:T(8,128)S(1)}, f32[2,16,256,64]{2,3,1,0:T(8,128)}, s32[1024]{0:T(1024)S(1)},...) while((s32[]{:T(128)}, f32[2,16,256]{2,1,0:T(8,128)S(1)}, ...), condition=%wide.region_12.13_spmd, body=%wide.region_3.12_spmd.sunk | while | flops 1130135552 | bytes 103557752 | solution.py:73
  170.5 3.1 %slice_bitcast_fusion.9 = (f32[16,256,64]{1,2,0:T(8,128)}, f32[16,256,64]{1,2,0:T(8,128)}) fusion(f32[2,16,256,64]{2,3,1,0:T(8,128)} %get-tuple-element.491), kind=kLoop, calls=%fused_computation.38.clone.1 | loop fusion | bytes 4194304 | tf_op jit(solution)/shard_map/while/body/eval_jaxpr/squeeze | solution.py:54
  173.6 3.0 %constant_dynamic-slice_fusion.3 = (bf16[512,1024]{1,0:T(8,128)(2,1)}, bf16[512,1024]{1,0:T(8,128)(2,1)}) fusion(bf16[1024,1024]{1,0:T(8,128)(2,1)} %get-tuple-element.509, s32[]{:T(128)S(6)} %select_n.71, bf16[1024,1024]{1,0:T(8,128)(2,1)} %get-tuple-element.508), kind=kLoop, calls=%fused_computation.45.clone.1 | loop fusion | bytes 4194308 | tf_op jit(solution)/shard_map/while/body/eval_jaxpr/dynamic_slice | solution.py:48
  181.1 11.9 %conditional.4 = (f32[1,16,256]{2,1,0:T(8,128)}, f32[1,16,256]{2,1,0:T(8,128)S(1)}, f32[1,16,256,64]{2,3,1,0:T(8,128)}) conditional(s32[]{:T(128)} %bitcast.100, (f32[16,256]{1,0:T(8,128)}, f32[16,256]{1,0:T(8,128)S(1)}, f32[16,256,64]{1,2,0:T(8,128)}) %tuple.134, (s32[512]{0:T(512)S(1)}, s32[256]{0:T(256)S(1)}, bf16[2,256,16,64]{1,3,2,0:T(8,128)(2,1)}, ...), branch_computations={%region_8.8_spmd, %region_9.0_spmd} | conditional | flops 564797440 | bytes 43224172 | solution.py:70
  181.2 2.9 %fusion.18 = (f32[16,256]{1,0:T(8,128)S(1)}, f32[16,256,512]{2,1,0:T(8,128)S(1)}) fusion(pred[256,512]{1,0:T(8,128)(4,1)S(1)} %broadcast_compare_fusion.1, bf16[512,16,64]{0,2,1:T(8,128)(2,1)S(1)} %get-tuple-element.254, bf16[2,256,16,64]{1,3,2,0:T(8,128)(2,1)} %get-tuple-element.253), kind=kOutput, calls=%fused_computation.20 | convolution fusion | flops 274722816 | bytes 10108928 | tf_op jit(solution)/shard_map/while/body/eval_jaxpr/cond/branch_1_fun/rhd,khd->hrk/dot_general | solution.py:21
  184.8 3.2 %fusion.20 = f32[16,256]{1,0:T(8,128)S(1)} fusion(f32[16,256,512]{2,1,0:T(8,128)S(1)} %get-tuple-element.348, f32[16,256]{1,0:T(8,128)} %max.5, pred[256,512]{1,0:T(8,128)(4,1)S(1)} %broadcast_compare_fusion.1), kind=kLoop, calls=%fused_computation.22 | loop fusion | flops 10481664 | bytes 8552448 | tf_op jit(solution)/shard_map/while/body/eval_jaxpr/cond/branch_1_fun/reduce_sum | solution.py:29
  188.7 3.1 %fusion.27 = f32[1,16,256,64]{2,3,1,0:T(8,128)S(1)} fusion(bf16[512,16,64]{0,2,1:T(8,128)(2,1)S(1)} %copy-done.5, f32[16,256,512]{2,1,0:T(8,128)S(1)} %get-tuple-element.348, f32[16,256]{1,0:T(8,128)} %max.5, pred[256,512]{1,0:T(8,128)(4,1)S(1)} %broadcast_compare_fusion.1, f32[16,256,64]{1,2,0:T(8,128)S(1)} %copy-done.3, f32[16,256]{1,0:T(8,128)S(1)} %get-tuple-element.344), kind=kOutput, calls=%fused_computation.26 | convolution fusion | flops 279445504 | bytes 11698176 | tf_op jit(solution)/shard_map/while/body/eval_jaxpr/cond/branch_1_fun/hrk,khd->hrd/dot_general | solution.py:30
  195.4 11.8 %conditional.5 = (f32[1,16,256]{2,1,0:T(8,128)}, f32[1,16,256]{2,1,0:T(8,128)S(1)}, f32[1,16,256,64]{2,3,1,0:T(8,128)}) conditional(s32[]{:T(128)} %bitcast.103, (f32[16,256]{1,0:T(8,128)}, f32[16,256]{1,0:T(8,128)S(1)}, f32[16,256,64]{1,2,0:T(8,128)}) %tuple.136, (s32[512]{0:T(512)S(1)}, s32[256]{0:T(256)S(1)}, bf16[2,256,16,64]{1,3,2,0:T(8,128)(2,1)}, ...), branch_computations={%region_4.4_spmd, %region_5.0_spmd} | conditional | flops 564797440 | bytes 43224172 | solution.py:70
  195.6 2.9 %fusion = (f32[16,256]{1,0:T(8,128)S(1)}, f32[16,256,512]{2,1,0:T(8,128)S(1)}) fusion(pred[256,512]{1,0:T(8,128)(4,1)S(1)} %broadcast_compare_fusion, bf16[512,16,64]{0,2,1:T(8,128)(2,1)S(1)} %get-tuple-element.246, bf16[2,256,16,64]{1,3,2,0:T(8,128)(2,1)} %get-tuple-element.245), kind=kOutput, calls=%fused_computation.2 | convolution fusion | flops 274722816 | bytes 10108928 | tf_op jit(solution)/shard_map/while/body/eval_jaxpr/cond/branch_1_fun/rhd,khd->hrk/dot_general | solution.py:21
  199.1 3.2 %fusion.2 = f32[16,256]{1,0:T(8,128)S(1)} fusion(f32[16,256,512]{2,1,0:T(8,128)S(1)} %get-tuple-element.346, f32[16,256]{1,0:T(8,128)} %max.4, pred[256,512]{1,0:T(8,128)(4,1)S(1)} %broadcast_compare_fusion), kind=kLoop, calls=%fused_computation.4 | loop fusion | flops 10481664 | bytes 8552448 | tf_op jit(solution)/shard_map/while/body/eval_jaxpr/cond/branch_1_fun/reduce_sum | solution.py:29
  203.1 3.1 %fusion.9 = f32[1,16,256,64]{2,3,1,0:T(8,128)S(1)} fusion(bf16[512,16,64]{0,2,1:T(8,128)(2,1)S(1)} %copy-done.6, f32[16,256,512]{2,1,0:T(8,128)S(1)} %get-tuple-element.346, f32[16,256]{1,0:T(8,128)} %max.4, pred[256,512]{1,0:T(8,128)(4,1)S(1)} %broadcast_compare_fusion, f32[16,256,64]{1,2,0:T(8,128)S(1)} %copy-done.1, f32[16,256]{1,0:T(8,128)S(1)} %get-tuple-element.342), kind=kOutput, calls=%fused_computation.8 | convolution fusion | flops 279445504 | bytes 11698176 | tf_op jit(solution)/shard_map/while/body/eval_jaxpr/cond/branch_1_fun/hrk,khd->hrd/dot_general | solution.py:30
  208.0 3.1 %pad_maximum_fusion.8 = f32[2,16,256,64]{2,3,1,0:T(8,128)} fusion(f32[1,16,256,64]{2,3,1,0:T(8,128)} %get-tuple-element.460, f32[1,16,256,64]{2,3,1,0:T(8,128)} %get-tuple-element.461), kind=kLoop, calls=%fused_computation.36.clone.1 | loop fusion | flops 524288 | bytes 4194304 | tf_op jit(solution)/shard_map/while/body/eval_jaxpr/stack | solution.py:71
  214.1 3.1 %slice_bitcast_fusion.9 = (f32[16,256,64]{1,2,0:T(8,128)}, f32[16,256,64]{1,2,0:T(8,128)}) fusion(f32[2,16,256,64]{2,3,1,0:T(8,128)} %get-tuple-element.491), kind=kLoop, calls=%fused_computation.38.clone.1 | loop fusion | bytes 4194304 | tf_op jit(solution)/shard_map/while/body/eval_jaxpr/squeeze | solution.py:54
  217.2 3.0 %constant_dynamic-slice_fusion.3 = (bf16[512,1024]{1,0:T(8,128)(2,1)}, bf16[512,1024]{1,0:T(8,128)(2,1)}) fusion(bf16[1024,1024]{1,0:T(8,128)(2,1)} %get-tuple-element.509, s32[]{:T(128)S(6)} %select_n.71, bf16[1024,1024]{1,0:T(8,128)(2,1)} %get-tuple-element.508), kind=kLoop, calls=%fused_computation.45.clone.1 | loop fusion | bytes 4194308 | tf_op jit(solution)/shard_map/while/body/eval_jaxpr/dynamic_slice | solution.py:48
  224.7 11.9 %conditional.4 = (f32[1,16,256]{2,1,0:T(8,128)}, f32[1,16,256]{2,1,0:T(8,128)S(1)}, f32[1,16,256,64]{2,3,1,0:T(8,128)}) conditional(s32[]{:T(128)} %bitcast.100, (f32[16,256]{1,0:T(8,128)}, f32[16,256]{1,0:T(8,128)S(1)}, f32[16,256,64]{1,2,0:T(8,128)}) %tuple.134, (s32[512]{0:T(512)S(1)}, s32[256]{0:T(256)S(1)}, bf16[2,256,16,64]{1,3,2,0:T(8,128)(2,1)}, ...), branch_computations={%region_8.8_spmd, %region_9.0_spmd} | conditional | flops 564797440 | bytes 43224172 | solution.py:70
  224.8 2.9 %fusion.18 = (f32[16,256]{1,0:T(8,128)S(1)}, f32[16,256,512]{2,1,0:T(8,128)S(1)}) fusion(pred[256,512]{1,0:T(8,128)(4,1)S(1)} %broadcast_compare_fusion.1, bf16[512,16,64]{0,2,1:T(8,128)(2,1)S(1)} %get-tuple-element.254, bf16[2,256,16,64]{1,3,2,0:T(8,128)(2,1)} %get-tuple-element.253), kind=kOutput, calls=%fused_computation.20 | convolution fusion | flops 274722816 | bytes 10108928 | tf_op jit(solution)/shard_map/while/body/eval_jaxpr/cond/branch_1_fun/rhd,khd->hrk/dot_general | solution.py:21
  228.4 3.2 %fusion.20 = f32[16,256]{1,0:T(8,128)S(1)} fusion(f32[16,256,512]{2,1,0:T(8,128)S(1)} %get-tuple-element.348, f32[16,256]{1,0:T(8,128)} %max.5, pred[256,512]{1,0:T(8,128)(4,1)S(1)} %broadcast_compare_fusion.1), kind=kLoop, calls=%fused_computation.22 | loop fusion | flops 10481664 | bytes 8552448 | tf_op jit(solution)/shard_map/while/body/eval_jaxpr/cond/branch_1_fun/reduce_sum | solution.py:29
  232.4 3.2 %fusion.27 = f32[1,16,256,64]{2,3,1,0:T(8,128)S(1)} fusion(bf16[512,16,64]{0,2,1:T(8,128)(2,1)S(1)} %copy-done.5, f32[16,256,512]{2,1,0:T(8,128)S(1)} %get-tuple-element.348, f32[16,256]{1,0:T(8,128)} %max.5, pred[256,512]{1,0:T(8,128)(4,1)S(1)} %broadcast_compare_fusion.1, f32[16,256,64]{1,2,0:T(8,128)S(1)} %copy-done.3, f32[16,256]{1,0:T(8,128)S(1)} %get-tuple-element.344), kind=kOutput, calls=%fused_computation.26 | convolution fusion | flops 279445504 | bytes 11698176 | tf_op jit(solution)/shard_map/while/body/eval_jaxpr/cond/branch_1_fun/hrk,khd->hrd/dot_general | solution.py:30
  239.0 11.8 %conditional.5 = (f32[1,16,256]{2,1,0:T(8,128)}, f32[1,16,256]{2,1,0:T(8,128)S(1)}, f32[1,16,256,64]{2,3,1,0:T(8,128)}) conditional(s32[]{:T(128)} %bitcast.103, (f32[16,256]{1,0:T(8,128)}, f32[16,256]{1,0:T(8,128)S(1)}, f32[16,256,64]{1,2,0:T(8,128)}) %tuple.136, (s32[512]{0:T(512)S(1)}, s32[256]{0:T(256)S(1)}, bf16[2,256,16,64]{1,3,2,0:T(8,128)(2,1)}, ...), branch_computations={%region_4.4_spmd, %region_5.0_spmd} | conditional | flops 564797440 | bytes 43224172 | solution.py:70
  239.2 2.9 %fusion = (f32[16,256]{1,0:T(8,128)S(1)}, f32[16,256,512]{2,1,0:T(8,128)S(1)}) fusion(pred[256,512]{1,0:T(8,128)(4,1)S(1)} %broadcast_compare_fusion, bf16[512,16,64]{0,2,1:T(8,128)(2,1)S(1)} %get-tuple-element.246, bf16[2,256,16,64]{1,3,2,0:T(8,128)(2,1)} %get-tuple-element.245), kind=kOutput, calls=%fused_computation.2 | convolution fusion | flops 274722816 | bytes 10108928 | tf_op jit(solution)/shard_map/while/body/eval_jaxpr/cond/branch_1_fun/rhd,khd->hrk/dot_general | solution.py:21
  242.7 3.2 %fusion.2 = f32[16,256]{1,0:T(8,128)S(1)} fusion(f32[16,256,512]{2,1,0:T(8,128)S(1)} %get-tuple-element.346, f32[16,256]{1,0:T(8,128)} %max.4, pred[256,512]{1,0:T(8,128)(4,1)S(1)} %broadcast_compare_fusion), kind=kLoop, calls=%fused_computation.4 | loop fusion | flops 10481664 | bytes 8552448 | tf_op jit(solution)/shard_map/while/body/eval_jaxpr/cond/branch_1_fun/reduce_sum | solution.py:29
  246.7 3.1 %fusion.9 = f32[1,16,256,64]{2,3,1,0:T(8,128)S(1)} fusion(bf16[512,16,64]{0,2,1:T(8,128)(2,1)S(1)} %copy-done.6, f32[16,256,512]{2,1,0:T(8,128)S(1)} %get-tuple-element.346, f32[16,256]{1,0:T(8,128)} %max.4, pred[256,512]{1,0:T(8,128)(4,1)S(1)} %broadcast_compare_fusion, f32[16,256,64]{1,2,0:T(8,128)S(1)} %copy-done.1, f32[16,256]{1,0:T(8,128)S(1)} %get-tuple-element.342), kind=kOutput, calls=%fused_computation.8 | convolution fusion | flops 279445504 | bytes 11698176 | tf_op jit(solution)/shard_map/while/body/eval_jaxpr/cond/branch_1_fun/hrk,khd->hrd/dot_general | solution.py:30
  251.6 3.1 %pad_maximum_fusion.8 = f32[2,16,256,64]{2,3,1,0:T(8,128)} fusion(f32[1,16,256,64]{2,3,1,0:T(8,128)} %get-tuple-element.460, f32[1,16,256,64]{2,3,1,0:T(8,128)} %get-tuple-element.461), kind=kLoop, calls=%fused_computation.36.clone.1 | loop fusion | flops 524288 | bytes 4194304 | tf_op jit(solution)/shard_map/while/body/eval_jaxpr/stack | solution.py:71
  (111 shorter events, 46.6 us)
Async XLA Ops:
  6.5 251.3 %copy-start = (bf16[1024,1024]{1,0:T(8,128)(2,1)S(1)}, bf16[1024,1024]{1,0:T(8,128)(2,1)}, u32[]{:S(2)}) copy-start(bf16[1024,1024]{1,0:T(8,128)(2,1)} %param.24) | copy-start | bytes 6291460
  6.5 30.7 %copy-start.10 = (bf16[1024]{0:T(1024)(128)(2,1)S(1)}, bf16[1024]{0:T(1024)(128)(2,1)}, u32[]{:S(2)}) copy-start(bf16[1024]{0:T(1024)(128)(2,1)} %param.20) | copy-start | bytes 6148
  31.0 28.5 %all-to-all-start.1 = ((bf16[8,1,128,512]{2,3,1,0:T(8,128)(2,1)}), bf16[8,1,128,512]{2,3,1,0:T(8,128)(2,1)S(1)}, u32[]{:S(2)}, u32[]{:S(2)}) async-start(bf16[8,1,128,512]{2,3,1,0:T(8,128)(2,1)} %bitcast_dynamic-update-slice_fusion), calls=%async_computation.1 | async-start | bytes 2097152 | tf_op jit(solution)/shard_map/all_to_all | solution.py:95
  37.2 78.9 %all-gather.3.cloned.1.call-start = ((), (), s32[]{:S(2)}) async-start(), calls=%async_computation.2 | async-start | bytes 2359296 | tf_op jit(solution)/shard_map/all_gather | solution.py:122
  59.5 5.7 %copy-start.8 = (bf16[1024,1024]{1,0:T(8,128)(2,1)S(1)}, bf16[1024,1024]{1,0:T(8,128)(2,1)}, u32[]{:S(2)}) copy-start(bf16[1024,1024]{1,0:T(8,128)(2,1)} %param.22) | copy-start | bytes 6291460
  59.5 10.0 %copy-start.9 = (s32[1,1024]{1,0:T(1,128)S(1)}, s32[1,1024]{1,0:T(1,128)}, u32[]{:S(2)}) copy-start(s32[1,1024]{1,0:T(1,128)} %param.18) | copy-start | bytes 12292
  64.4 0.8 copy-start.7
  66.4 12.5 %copy-start.11 = (bf16[1024]{0:T(1024)(128)(2,1)S(1)}, bf16[1024]{0:T(1024)(128)(2,1)}, u32[]{:S(2)}) copy-start(bf16[1024]{0:T(1024)(128)(2,1)} %param.25) | copy-start | bytes 6148
  66.4 99.4 %all-gather.5.cloned.1.call-start = ((), (), s32[]{:S(2)}) async-start(), calls=%async_computation.3 | async-start | bytes 2359296 | tf_op jit(solution)/shard_map/all_gather | solution.py:123
  181.2 7.5 %copy-start.3 = (f32[16,256,64]{1,2,0:T(8,128)S(1)}, f32[16,256,64]{1,2,0:T(8,128)}, u32[]{:S(2)}) copy-start(f32[16,256,64]{1,2,0:T(8,128)} %get-tuple-element.256) | copy-start | bytes 3145732 | tf_op jit(solution)/shard_map/while/body/eval_jaxpr/cond
  181.2 7.5 %copy-start.5 = (bf16[512,16,64]{0,2,1:T(8,128)(2,1)S(1)}, bf16[512,16,64]{0,2,1:T(8,128)(2,1)}, u32[]{:S(2)}) copy-start(bf16[512,16,64]{0,2,1:T(8,128)(2,1)} %get-tuple-element.257) | copy-start | bytes 3145732 | tf_op jit(solution)/shard_map/while/body/eval_jaxpr/cond
  191.9 1.0 copy-start.4
  195.5 7.5 %copy-start.1 = (f32[16,256,64]{1,2,0:T(8,128)S(1)}, f32[16,256,64]{1,2,0:T(8,128)}, u32[]{:S(2)}) copy-start(f32[16,256,64]{1,2,0:T(8,128)} %get-tuple-element.248) | copy-start | bytes 3145732 | tf_op jit(solution)/shard_map/while/body/eval_jaxpr/cond
  195.6 7.5 %copy-start.6 = (bf16[512,16,64]{0,2,1:T(8,128)(2,1)S(1)}, bf16[512,16,64]{0,2,1:T(8,128)(2,1)}, u32[]{:S(2)}) copy-start(bf16[512,16,64]{0,2,1:T(8,128)(2,1)} %get-tuple-element.249) | copy-start | bytes 3145732 | tf_op jit(solution)/shard_map/while/body/eval_jaxpr/cond
  206.2 1.0 copy-start.2
  224.8 7.5 %copy-start.3 = (f32[16,256,64]{1,2,0:T(8,128)S(1)}, f32[16,256,64]{1,2,0:T(8,128)}, u32[]{:S(2)}) copy-start(f32[16,256,64]{1,2,0:T(8,128)} %get-tuple-element.256) | copy-start | bytes 3145732 | tf_op jit(solution)/shard_map/while/body/eval_jaxpr/cond
  224.8 7.5 %copy-start.5 = (bf16[512,16,64]{0,2,1:T(8,128)(2,1)S(1)}, bf16[512,16,64]{0,2,1:T(8,128)(2,1)}, u32[]{:S(2)}) copy-start(bf16[512,16,64]{0,2,1:T(8,128)(2,1)} %get-tuple-element.257) | copy-start | bytes 3145732 | tf_op jit(solution)/shard_map/while/body/eval_jaxpr/cond
  235.5 1.0 copy-start.4
  239.2 7.5 %copy-start.1 = (f32[16,256,64]{1,2,0:T(8,128)S(1)}, f32[16,256,64]{1,2,0:T(8,128)}, u32[]{:S(2)}) copy-start(f32[16,256,64]{1,2,0:T(8,128)} %get-tuple-element.248) | copy-start | bytes 3145732 | tf_op jit(solution)/shard_map/while/body/eval_jaxpr/cond
  239.2 7.5 %copy-start.6 = (bf16[512,16,64]{0,2,1:T(8,128)(2,1)S(1)}, bf16[512,16,64]{0,2,1:T(8,128)(2,1)}, u32[]{:S(2)}) copy-start(bf16[512,16,64]{0,2,1:T(8,128)(2,1)} %get-tuple-element.249) | copy-start | bytes 3145732 | tf_op jit(solution)/shard_map/while/body/eval_jaxpr/cond
  249.9 1.0 copy-start.2
Sparse Core Ops, SparseCore 0:
  66.5 49.5 all-gather.2
  118.2 47.6 all-gather.4
